TPU v7x, 256 devices: a 4x2x16 block of a 4x16x16 slice. The times are simulated.
256 devices in a mesh: groups: 2 (over y), mp: 16 (over z), expert: 4 (over x), dp: 2 (over core).
Axes of the slice: x: 4, y: 2, z: 16, core: 2. Of those that a mesh axis runs over, the one named last changes fastest.
The devices are a block of a 4x16x16 slice.
Arguments:
- hidden_in: bfloat16 [1024, 4096], P(('groups', 'expert', 'dp'), 'mp'), parts along dimension 0, may hold values from -6 to 6
- norm_gain: bfloat16 [2, 4096], P(None, 'mp'), may hold values from 0.25 to 1.75
- expert_ids: int32 [2, 1024, 2], P(None, ('groups', 'expert', 'dp')), parts along dimension 1, may hold values from 0 to 3, all different within a row; in each aligned block of 64 rows (0 to 63, 64 to 127, ..., all dimensions but the last counted through in order) at most 64 rows name the same one
- gate_counts: int32 [2, 1024, 2], P(None, ('groups', 'expert', 'dp')), parts along dimension 1, may hold values from 8 to 15
- exit_layer: int32 [1024], P(('groups', 'expert', 'dp')), parts along dimension 0, may hold values from 1 to 2
- w_gate: bfloat16 [2, 4, 7168, 4096], P(None, 'expert', ('mp', 'dp')), may hold values from -0.09375 to 0.09375
- w_up: bfloat16 [2, 4, 7168, 4096], P(None, 'expert', ('mp', 'dp')), may hold values from -0.09375 to 0.09375
- w_down: bfloat16 [2, 4, 7168, 4096], P(None, 'expert', ('mp', 'dp')), may hold values from -0.0625 to 0.0625
Outputs:
- hidden_out: bfloat16 [1024, 4096], P(('groups', 'expert', 'dp'), 'mp'), parts along dimension 0
There are 2 independent parts, one for each index of `groups`. A program takes and returns all parts, laid end to end along the dimension named above; an argument that names none is the same for every part. Nothing has to cross between parts.
Inputs may be any that keep to these rules, and one draw needn't show every extreme that they name: `expert_ids`: A token's two ids in a layer differ. In the rows of one device in one layer (aligned blocks of 64 rows, layer by layer) some expert may be named by all 64 rows.
All inputs are finite; a program needn't handle non-finite values.
Results may differ from a plain program's by a relative error of at most 0.014.
Values may be sent and summed in bfloat16 or wider, within the bound.
A program may use at most 128 MiB of HBM per device.

v0:
```python
import jax
import jax.numpy as jnp
from jax import lax
from jax.sharding import PartitionSpec as P

LAYERS = 2


norm_floor = 0.1


def rows_first(arrays, axis, dims):
    turned = [jnp.moveaxis(a, dim, 0) for a, dim in zip(arrays, dims)]
    both = jnp.concatenate([t.reshape(len(t), -1) for t in turned], axis=1)
    whole, at, outs = (lax.all_gather(both, axis, axis=0, tiled=True), 0, [])
    for t, dim in zip(turned, dims):
        section = whole[:, at : at + t[0].size].reshape(-1, *t.shape[1:])
        outs.append(jnp.moveaxis(section, 0, dim))
        at += t[0].size
    return tuple(outs)


def side_by_side(arrays, axis, dim, along):
    ends, at = ([], 0)
    for a in arrays[:-1]:
        at += a.shape[along]
        ends.append(at)
    both = jnp.concatenate(arrays, axis=along)
    return tuple(jnp.split(lax.all_gather(both, axis, axis=dim, tiled=True), ends, axis=along))


def body(hidden_in, norm_gain, expert_ids, gate_counts, exit_layer, w_gate, w_up, w_down):
    experts = lax.axis_size("expert")
    shards = lax.axis_size("mp")
    tok_rows, slice_width = hidden_in.shape
    full_width = slice_width * shards
    contract = (((1,), (1,)), ((), ()))
    expert_range = jnp.arange(experts, dtype=jnp.int32)
    slot_range = jnp.arange(tok_rows, dtype=jnp.int32)
    current = hidden_in
    for layer_idx in range(LAYERS):
        counts = gate_counts[layer_idx].astype(jnp.float32)
        gate_share = counts / jnp.sum(counts, axis=1, keepdims=True)
        active = exit_layer > layer_idx
        matched = (expert_ids[layer_idx][:, :, None] == expert_range[None, None, :]) & active[
            :, None, None
        ]
        chosen = jnp.sum(matched.astype(jnp.int32), axis=1)
        weight_te = jnp.sum(jnp.where(matched, gate_share[:, :, None], jnp.float32(0.0)), axis=1)
        slot_rank = jnp.cumsum(chosen, axis=0) - chosen
        place_mask = (slot_rank.T[:, None, :] == slot_range[None, :, None]) & (
            chosen.T[:, None, :] > 0
        )
        place_bf = place_mask.astype(jnp.bfloat16)
        current_f32 = current.astype(jnp.float32)
        whole_rows, whole_gain = rows_first((current, norm_gain[layer_idx]), "mp", (1, 0))
        whole_f32 = whole_rows.astype(jnp.float32)
        sum_squares = jnp.sum(whole_f32 * whole_f32, axis=1)
        inv_rms = lax.rsqrt(sum_squares / full_width + norm_floor)
        normed = (whole_f32 * inv_rms[:, None] * whole_gain.astype(jnp.float32)[None, :]).astype(
            jnp.bfloat16
        )
        outgoing = jnp.einsum(
            "ect,td->ecd", place_bf, normed, preferred_element_type=jnp.float32
        ).astype(jnp.bfloat16)
        incoming = lax.all_to_all(outgoing, "expert", split_axis=0, concat_axis=0, tiled=True)
        inputs = incoming.reshape(experts * tok_rows, full_width)
        gate_rows, up_rows, down_rows = side_by_side(
            (w_gate[layer_idx, 0], w_up[layer_idx, 0], w_down[layer_idx, 0]), "dp", 0, 1
        )
        gate_val = lax.dot_general(inputs, gate_rows, contract, preferred_element_type=jnp.float32)
        up_val = lax.dot_general(inputs, up_rows, contract, preferred_element_type=jnp.float32)
        hidden = (jax.nn.silu(gate_val) * up_val).astype(jnp.bfloat16)
        partial_value = jnp.dot(hidden, down_rows, preferred_element_type=jnp.float32)
        summed = lax.psum_scatter(
            partial_value.astype(jnp.bfloat16), "mp", scatter_dimension=1, tiled=True
        )
        returned = lax.all_to_all(
            summed.reshape(experts, tok_rows, slice_width),
            "expert",
            split_axis=0,
            concat_axis=0,
            tiled=True,
        )
        place_weight = place_mask.astype(jnp.float32) * weight_te.T[:, None, :]
        update = jnp.einsum("ect,ecd->td", place_weight, returned.astype(jnp.float32))
        current = (current_f32 + update).astype(jnp.bfloat16)
    return current


def solution(mesh):
    in_specs = (
        P(("groups", "expert", "dp"), "mp"),
        P(None, "mp"),
        P(None, ("groups", "expert", "dp"), None),
        P(None, ("groups", "expert", "dp"), None),
        P(("groups", "expert", "dp")),
        P(None, "expert", ("mp", "dp"), None),
        P(None, "expert", ("mp", "dp"), None),
        P(None, "expert", ("mp", "dp"), None),
    )
    out_specs = P(("groups", "expert", "dp"), "mp")
    return jax.shard_map(body, mesh=mesh, in_specs=in_specs, out_specs=out_specs, check_vma=False)
```

profile of v0, /device:TPU:40, one launch (start us, length us, event | category | flops | bytes accessed | tf_op | source)
XLA Modules:
  0.0 336.3 jit_solution(16841984590572916138)
XLA Ops:
  6.5 0.0 all-gather.3.cloned.1.call-start
  6.6 0.0 copy-start
  6.6 2.5 slice_bitcast_fusion.5
  9.1 0.6 copy-done
  9.7 1.1 copy-done.1
  10.8 2.8 slice_bitcast_fusion.3
  13.6 5.6 %pad_maximum_fusion = bf16[224,12288]{1,0:T(8,128)(2,1)} fusion(bf16[224,4096]{1,0:T(8,128)(2,1)S(1)} %get-tuple-element.11, bf16[224,4096]{1,0:T(8,128)(2,1)S(1)} %get-tuple-element.22, bf16[224,4096]{1,0:T(8,128)(2,1)S(1)} %get-tuple-element.7), kind=kLoop, calls=%fused_computation | loop fusion | flops 16515072 | bytes 11010048 | tf_op jit(solution)/shard_map/concatenate | solution.py:28
  19.1 0.1 all-gather.3.cloned.1.call-update
  19.2 0.1 reduce-scatter.3.cloned.1.call-start
  19.3 0.5 copy-done.6
  19.8 0.0 copy-done.5
  19.8 0.1 copy.19
  19.9 0.1 reduce_window_sum.17
  20.0 0.1 copy.21
  20.1 0.0 copy-done.4
  20.1 0.0 copy-done.2
  20.2 51.8 %all_gather.12 = bf16[4096,65]{0,1:T(8,128)(2,1)S(1)} all-gather(bf16[256,65]{0,1:T(8,128)(2,1)S(1)} %pad_maximum_fusion.2), channel_id=1, replica_groups=mesh['groups'=2,'mp'=16,'expert'=4,'dp'=2] {'mp'}, dimensions={0}, use_global_device_ids=true | all-gather | bytes 565760 | tf_op jit(solution)/shard_map/all_gather | solution.py:15
  72.0 0.2 fusion.30
  72.2 0.9 convolution_convert_fusion.3
  73.1 23.9 %all_to_all.20 = bf16[4,64,4096]{2,1,0:T(8,128)(2,1)} all-to-all(bf16[4,64,4096]{2,1,0:T(8,128)(2,1)S(1)} %convolution_convert_fusion.3), channel_id=1, replica_groups=mesh['groups'=2,'mp'=16,'expert'=4,'dp'=2] {'expert'}, dimensions={0} | all-to-all | bytes 4194304 | tf_op jit(solution)/shard_map/all_to_all | solution.py:66
  97.0 3.8 %fusion.8 = f32[256,448]{0,1:T(8,128)S(1)} fusion(bf16[256,4096]{1,0:T(8,128)(2,1)} %bitcast.68, bf16[448,12288]{1,0:T(8,128)(2,1)} %all-gather.3.cloned.1.call-done), kind=kOutput, calls=%fused_computation.14 | convolution fusion | flops 939524096 | bytes 6225920 | tf_op jit(solution)/shard_map/dot_general | solution.py:71
  100.8 9.4 %convolution_convert_fusion.2 = bf16[256,4096]{1,0:T(8,128)(2,1)} fusion(bf16[448,12288]{1,0:T(8,128)(2,1)} %all-gather.3.cloned.1.call-done, bf16[256,4096]{1,0:T(8,128)(2,1)} %bitcast.69, f32[256,448]{0,1:T(8,128)S(1)} %fusion.8), kind=kOutput, calls=%fused_computation.4 | convolution fusion | flops 1880784896 | bytes 11993088 | tf_op jit(solution)/shard_map/dot_general | solution.py:74
  110.2 0.1 reduce-scatter.3.cloned.1.call-update
  110.2 0.1 all-gather.5.cloned.1.call-start
  110.3 4.9 %pad_maximum_fusion.1 = bf16[224,12288]{1,0:T(8,128)(2,1)} fusion(bf16[224,4096]{1,0:T(8,128)(2,1)} %get-tuple-element.12, bf16[224,4096]{1,0:T(8,128)(2,1)} %get-tuple-element.21, bf16[224,4096]{1,0:T(8,128)(2,1)S(1)} %get-tuple-element.8), kind=kLoop, calls=%fused_computation.1 | loop fusion | flops 16515072 | bytes 11010048 | tf_op jit(solution)/shard_map/concatenate | solution.py:28
  115.2 0.1 all-gather.5.cloned.1.call-update
  115.3 0.1 copy.23
  115.4 0.1 reduce_window_sum.18
  115.5 0.1 copy.25
  115.6 0.3 copy-done.3
  115.9 57.0 %reduce-scatter.3.cloned.1.call-done = bf16[256,256]{1,0:T(8,128)(2,1)} async-done(((bf16[256,4096]{1,0:T(8,128)(2,1)}), bf16[256,256]{1,0:T(8,128)(2,1)}) %reduce-scatter.3.cloned.1.call-update) | async-done | bytes 131088 | tf_op jit(solution)/shard_map/reduce_scatter | solution.py:75
  172.9 4.3 %all-to-all-start.1 = ((bf16[4,64,256]{2,1,0:T(8,128)(2,1)}), bf16[4,64,256]{2,1,0:T(8,128)(2,1)S(1)}, u32[]{:S(2)}, u32[]{:S(2)}) async-start(bf16[4,64,256]{2,1,0:T(8,128)(2,1)} %bitcast.70), calls=%async_computation.2 | async-start | bytes 262144 | tf_op jit(solution)/shard_map/all_to_all | solution.py:78
  177.3 6.0 %all-to-all-done.1 = bf16[4,64,256]{2,1,0:T(8,128)(2,1)S(1)} async-done(((bf16[4,64,256]{2,1,0:T(8,128)(2,1)}), bf16[4,64,256]{2,1,0:T(8,128)(2,1)S(1)}, u32[]{:S(2)}, u32[]{:S(2)}) %all-to-all-start.1) | async-done | bytes 131104 | tf_op jit(solution)/shard_map/all_to_all | solution.py:78
  183.2 0.3 fusion.29
  183.5 30.7 %all_gather.14 = bf16[4096,65]{0,1:T(8,128)(2,1)S(1)} all-gather(bf16[256,65]{0,1:T(8,128)(2,1)S(1)} %pad_maximum_fusion.3), channel_id=1, replica_groups=mesh['groups'=2,'mp'=16,'expert'=4,'dp'=2] {'mp'}, dimensions={0}, use_global_device_ids=true | all-gather | bytes 565760 | tf_op jit(solution)/shard_map/all_gather | solution.py:15
  214.3 0.2 fusion.33
  214.5 2.2 convolution_convert_fusion.1
  216.7 3.7 %all-to-all-start.2 = ((bf16[4,64,4096]{2,1,0:T(8,128)(2,1)}), bf16[4,64,4096]{2,1,0:T(8,128)(2,1)S(1)}, u32[]{:S(2)}, u32[]{:S(2)}) async-start(bf16[4,64,4096]{2,1,0:T(8,128)(2,1)} %convolution_convert_fusion.1), calls=%async_computation.3 | async-start | bytes 4194304 | tf_op jit(solution)/shard_map/all_to_all | solution.py:66
  220.4 0.2 reduce-scatter.5.cloned.1.call-start
  220.7 0.0 all-gather.5.cloned.1.call-done
  220.7 16.1 %all-to-all-done.2 = bf16[4,64,4096]{2,1,0:T(8,128)(2,1)S(1)} async-done(((bf16[4,64,4096]{2,1,0:T(8,128)(2,1)}), bf16[4,64,4096]{2,1,0:T(8,128)(2,1)S(1)}, u32[]{:S(2)}, u32[]{:S(2)}) %all-to-all-start.2) | async-done | bytes 2097184 | tf_op jit(solution)/shard_map/all_to_all | solution.py:66
  236.8 3.2 fusion.3
  240.0 8.8 %convolution_convert_fusion = bf16[256,4096]{1,0:T(8,128)(2,1)} fusion(bf16[448,12288]{1,0:T(8,128)(2,1)} %all-gather.5.cloned.1.call-done, bf16[256,4096]{1,0:T(8,128)(2,1)S(1)} %bitcast.67, f32[256,448]{0,1:T(8,128)S(1)} %fusion.3), kind=kOutput, calls=%fused_computation.2 | convolution fusion | flops 1880784896 | bytes 11993088 | tf_op jit(solution)/shard_map/dot_general | solution.py:74
  248.8 0.1 reduce-scatter.5.cloned.1.call-update
  248.9 69.8 %reduce-scatter.5.cloned.1.call-done = bf16[256,256]{1,0:T(8,128)(2,1)} async-done(((bf16[256,4096]{1,0:T(8,128)(2,1)}), bf16[256,256]{1,0:T(8,128)(2,1)}) %reduce-scatter.5.cloned.1.call-update) | async-done | bytes 131088 | tf_op jit(solution)/shard_map/reduce_scatter | solution.py:75
  318.7 4.2 %all-to-all-start.3 = ((bf16[4,64,256]{2,1,0:T(8,128)(2,1)}), bf16[4,64,256]{2,1,0:T(8,128)(2,1)S(1)}, u32[]{:S(2)}, u32[]{:S(2)}) async-start(bf16[4,64,256]{2,1,0:T(8,128)(2,1)} %bitcast.71), calls=%async_computation.5 | async-start | bytes 262144 | tf_op jit(solution)/shard_map/all_to_all | solution.py:78
  322.9 6.0 %all-to-all-done.3 = bf16[4,64,256]{2,1,0:T(8,128)(2,1)S(1)} async-done(((bf16[4,64,256]{2,1,0:T(8,128)(2,1)}), bf16[4,64,256]{2,1,0:T(8,128)(2,1)S(1)}, u32[]{:S(2)}, u32[]{:S(2)}) %all-to-all-start.3) | async-done | bytes 131104 | tf_op jit(solution)/shard_map/all_to_all | solution.py:78
  328.9 0.9 fusion.28
  (26 shorter events, 0.2 us)
Async XLA Ops:
  6.5 90.4 %all-gather.3.cloned.1.call-start = ((), (), s32[]{:S(2)}) async-start(), calls=%async_computation.6 | async-start | bytes 16515072 | tf_op jit(solution)/shard_map/all_gather | solution.py:29
  6.6 3.1 copy-start
  6.6 4.3 %copy-start.1 = (bf16[2,1,224,4096]{3,2,1,0:T(8,128)(2,1)S(1)}, bf16[2,1,224,4096]{3,2,1,0:T(8,128)(2,1)}, u32[]{:S(2)}) copy-start(bf16[2,1,224,4096]{3,2,1,0:T(8,128)(2,1)} %param.14) | copy-start | bytes 11010052
  19.1 0.7 copy-start.6
  19.1 0.7 copy-start.5
  19.1 1.0 copy-start.4
  19.1 1.0 copy-start.2
  19.2 153.7 %reduce-scatter.3.cloned.1.call-start = ((), (), s32[]{:S(2)}) async-start(), calls=%async_computation.7 | async-start | bytes 2228224 | tf_op jit(solution)/shard_map/reduce_scatter | solution.py:75
  110.2 110.5 %all-gather.5.cloned.1.call-start = ((), (), s32[]{:S(2)}) async-start(), calls=%async_computation.8 | async-start | bytes 16515072 | tf_op jit(solution)/shard_map/all_gather | solution.py:29
  115.2 0.7 copy-start.3
  172.9 10.3 %all-to-all-start.1 = ((bf16[4,64,256]{2,1,0:T(8,128)(2,1)}), bf16[4,64,256]{2,1,0:T(8,128)(2,1)S(1)}, u32[]{:S(2)}, u32[]{:S(2)}) async-start(bf16[4,64,256]{2,1,0:T(8,128)(2,1)} %bitcast.70), calls=%async_computation.2 | async-start | bytes 262144 | tf_op jit(solution)/shard_map/all_to_all | solution.py:78
  216.7 20.1 %all-to-all-start.2 = ((bf16[4,64,4096]{2,1,0:T(8,128)(2,1)}), bf16[4,64,4096]{2,1,0:T(8,128)(2,1)S(1)}, u32[]{:S(2)}, u32[]{:S(2)}) async-start(bf16[4,64,4096]{2,1,0:T(8,128)(2,1)} %convolution_convert_fusion.1), calls=%async_computation.3 | async-start | bytes 4194304 | tf_op jit(solution)/shard_map/all_to_all | solution.py:66
  220.4 98.3 %reduce-scatter.5.cloned.1.call-start = ((), (), s32[]{:S(2)}) async-start(), calls=%async_computation.9 | async-start | bytes 2228224 | tf_op jit(solution)/shard_map/reduce_scatter | solution.py:75
  318.7 10.2 %all-to-all-start.3 = ((bf16[4,64,256]{2,1,0:T(8,128)(2,1)}), bf16[4,64,256]{2,1,0:T(8,128)(2,1)S(1)}, u32[]{:S(2)}, u32[]{:S(2)}) async-start(bf16[4,64,256]{2,1,0:T(8,128)(2,1)} %bitcast.71), calls=%async_computation.5 | async-start | bytes 262144 | tf_op jit(solution)/shard_map/all_to_all | solution.py:78
Sparse Core Ops, SparseCore 0:
  19.3 45.2 all-gather.2
  110.4 62.5 reduce-scatter.2
  174.8 29.9 all-gather.4
  249.0 69.6 reduce-scatter.4
where the time goes:
time: 337 us; the launch traced here: 336 us
  waiting for transfers between devices  155 us (46%)
  blocking collectives  106 us (31%)
  matrix products  29.4 us (9%)
  between operations  13.3 us (4%)
  starting transfers between devices  12.6 us (4%)
  other arithmetic  11.3 us (3%)
  local copies, waits for them, and re-layouts  8.24 us (2%)
    reduce_scatter x2, waiting for transfers between devices, body(): lax.psum_scatter(partial_value.astype(jnp.bfloat16), 'mp', scatter_dimens...  127 us
    all_gather x2, blocking collectives, rows_first(): whole, at, outs = (lax.all_gather(both, axis, axis=0, tiled=True), 0, [])  82.5 us
    all_to_all x1, blocking collectives, body(): lax.all_to_all(outgoing, 'expert', split_axis=0, concat_axis=0, tiled=True)  23.9 us
    dot_general x2, matrix products, body(): jnp.dot(hidden, down_rows, preferred_element_type=jnp.float32)  18.2 us
    all_to_all x1, waiting for transfers between devices, body(): lax.all_to_all(outgoing, 'expert', split_axis=0, concat_axis=0, tiled=True)  16.1 us
    all_to_all x2, waiting for transfers between devices, body(): lax.all_to_all(summed.reshape(experts, tok_rows, slice_width), 'expert',...  11.9 us
    concatenate x2, other arithmetic, side_by_side(): both = jnp.concatenate(arrays, axis=along)  10.5 us
    all_to_all x2, starting transfers between devices, body(): lax.all_to_all(summed.reshape(experts, tok_rows, slice_width), 'expert',...  8.52 us
  transfers between devices with their start and end apart: 7, of which 5 were waited for; matrix products, arithmetic and copies ran while one was open for 3% of the time, Pallas kernels for 0%

commit v1 on v0

v1 whole, which is shorter than its diff:
```python
import jax
import jax.numpy as jnp
from jax import lax
from jax.experimental import pallas as pl
from jax.experimental.pallas import tpu as pltpu
from jax.sharding import PartitionSpec as P

LAYERS = 2
NORM_FLOOR = 0.1
MESH = pl.DeviceIdType.MESH

ORDER = (0, 1, -1, 4, -4, 2, -2, 7, -7, 3, -3, 5, -5, 6, -6, 8)
HUBS = (7, -7, 4, -4, 1, -1)
FORWARD = {1: (1,), -1: (-1,), 4: (1, -1), -4: (-1, 1), 7: (1, -1), -7: (1,)}
LEAVES = tuple(h + s for h in HUBS for s in FORWARD[h])
TO_HUB = {h + s: -s for h in HUBS for s in FORWARD[h]}
AG_LAG = (3, 6)
RS_LAG = (3, 6)


def kernel(
    cur_in, gain_in, ids_in, counts_in, exit_in, wg_hbm, wu_hbm, wd_hbm, out_ref,
    acts, gains, routes, wgu, wdn, acc, ssq, hid, part, xa, xb, stage, zleaf, zdest,
    zr, xr, gr, rr, xas, xbs, zls, zds, lw, rw, sw, sends,
):
    m, e, d = lax.axis_index("mp"), lax.axis_index("expert"), lax.axis_index("dp")
    n_mp, n_x = acts.shape[1], acts.shape[2]
    rows, width = cur_in.shape
    half = rows // 2
    tokens = n_x * rows
    hidden = 2 * wdn.shape[2]
    full = n_mp * width

    def z(step):
        return {"mp": lax.rem(m + (step + n_mp), n_mp)}

    def x(step):
        return {"expert": lax.rem(e + (step + n_x), n_x)}

    partner = {"dp": 1 - d}
    em, ep, eo = (lax.rem(e + s, n_x) for s in (n_x - 1, 1, 2))

    def owner(delta):
        return lax.rem(m + (n_mp - delta), n_mp)

    def send(src, dst, ssem, rsem, dev):
        pltpu.make_async_remote_copy(
            src_ref=src, dst_ref=dst, send_sem=ssem, recv_sem=rsem, device_id=dev, device_id_type=MESH
        ).start()

    def await_bytes(ref, sem):
        pltpu.make_async_copy(ref, ref, sem).wait()

    def weight_parts(layer):
        return (
            (wg_hbm.at[layer, 0], lambda s: wgu.at[layer, 0, s], 0),
            (wu_hbm.at[layer, 0], lambda s: wgu.at[layer, 1, s], 1),
            (wd_hbm.at[layer, 0], lambda s: wdn.at[layer, s], 2),
        )

    def load_weights(layer):
        for src, dst, j in weight_parts(layer):
            pltpu.make_async_copy(src, dst(0), lw.at[layer, j]).start()

    def give_weights(layer):
        for src, dst, j in weight_parts(layer):
            send(src, dst(1), sw.at[layer, j], rw.at[layer, j], partner)

    load_weights(0)

    lines = []
    for layer in range(LAYERS):
        counts = counts_in[layer].astype(jnp.float32)
        share = counts / jnp.sum(counts, axis=0, keepdims=True)
        active = exit_in[...] > layer
        for expert in range(n_x):
            named = jnp.where((ids_in[layer] == expert) & active, share, 0.0)
            lines.append(jnp.sum(named, axis=0, keepdims=True))
    routes[e, :, 0:rows] = jnp.concatenate(lines, axis=0)
    routes[e, :, rows:] = jnp.zeros((LAYERS * n_x, routes.shape[2] - rows), jnp.float32)
    gains[m] = gain_in[...].astype(jnp.float32)
    acts[0, m, e] = cur_in[...]

    barrier = pltpu.get_barrier_semaphore()
    peers = [z(h) for h in HUBS] + [x(1), x(-1), x(2), partner]
    for dev in peers:
        pl.semaphore_signal(barrier, inc=1, device_id=dev, device_id_type=MESH)
    pl.semaphore_wait(barrier, len(peers))

    def layer_step(layer, carry):
        own = acts.at[layer, m, e]
        for h in HUBS:
            send(own, own, sends.at[0], zr.at[layer, ORDER.index(h)], z(h))

        def spread(i):
            block = acts.at[layer, owner(ORDER[i]), e]
            send(block, block, sends.at[1], xr.at[layer, i, 0], x(1))
            send(block, block, sends.at[1], xr.at[layer, i, 1], x(-1))

        spread(0)

        @pl.when(layer == 0)
        def _():
            for h in HUBS:
                send(gains.at[m], gains.at[m], sends.at[2], gr.at[ORDER.index(h)], z(h))
            for j, s in enumerate((1, -1, 2)):
                send(routes.at[e], routes.at[e], sends.at[3], rr.at[j], x(s))
            give_weights(0)

        def take_z(i):
            delta = ORDER[i]
            k = owner(delta)
            block = acts.at[layer, k, e]
            await_bytes(block, zr.at[layer, i])
            for s in FORWARD.get(delta, ()):
                send(block, block, sends.at[0], zr.at[layer, ORDER.index(delta + s)], z(s))
            spread(i)

            @pl.when(layer == 0)
            def _():
                await_bytes(gains.at[k], gr.at[i])
                for s in FORWARD.get(delta, ()):
                    send(gains.at[k], gains.at[k], sends.at[2], gr.at[ORDER.index(delta + s)], z(s))

        def take_x(i):
            k = owner(ORDER[i])
            lo, hi = acts.at[layer, k, em], acts.at[layer, k, ep]
            await_bytes(lo, xr.at[layer, i, 0])
            piece = acts.at[layer, k, em, pl.ds(0, half)]
            send(piece, piece, sends.at[1], xr.at[layer, i, 2], x(1))
            await_bytes(hi, xr.at[layer, i, 1])
            piece = acts.at[layer, k, ep, pl.ds(half, half)]
            send(piece, piece, sends.at[1], xr.at[layer, i, 2], x(-1))

        def multiply(i):
            k = owner(ORDER[i])
            await_bytes(acts.at[layer, k, eo], xr.at[layer, i, 2])
            block = acts[layer, k].reshape(tokens, width).astype(jnp.float32)
            squares = block * block
            scaled = (block * gains[k, pl.ds(layer, 1), :]).astype(jnp.bfloat16)
            at = pl.ds(pl.multiple_of(k * width, width), width)
            ssq[...] = squares if i == 0 else ssq[...] + squares

            def product(j, c):
                w = wgu[layer, j, :, :, at].reshape(hidden, width)
                p = lax.dot_general(scaled, w, (((1,), (1,)), ((), ())), preferred_element_type=jnp.float32)
                acc[j] = p if i == 0 else acc[j] + p
                return c

            lax.fori_loop(0, 2, product, 0)

        def weights_here(j):
            await_bytes(wdn.at[layer, 0], lw.at[layer, j])
            await_bytes(wdn.at[layer, 1], rw.at[layer, j])

        for t in range(n_mp + AG_LAG[1]):
            if 0 < t < n_mp:
                take_z(t)
            if 0 <= t - AG_LAG[0] < n_mp:
                take_x(t - AG_LAG[0])
            if 0 <= t - AG_LAG[1] < n_mp:
                if t == AG_LAG[1]:
                    weights_here(0)
                    weights_here(1)
                multiply(t - AG_LAG[1])

        @pl.when(layer == 0)
        def _():
            for j, s in enumerate((em, ep, eo)):
                await_bytes(routes.at[s], rr.at[j])
            load_weights(1)
            give_weights(1)

        eye = lax.broadcasted_iota(jnp.int32, (rows, rows), 0) == lax.broadcasted_iota(jnp.int32, (rows, rows), 1)
        columns = []
        for s in range(n_x):
            line = routes[s, pl.ds(layer * n_x + e, 1), 0:rows]
            columns.append(jnp.sum(jnp.where(eye, line, 0.0), axis=1, keepdims=True))
        weight = jnp.concatenate(columns, axis=0)
        inv = lax.rsqrt(jnp.sum(ssq[...], axis=1, keepdims=True) / full + NORM_FLOOR)
        gate = acc[0] * inv
        hid[...] = (gate / (1.0 + jnp.exp(-gate)) * (acc[1] * inv) * weight).astype(jnp.bfloat16)
        weights_here(2)

        def down(i):
            f = owner(ORDER[i])
            at = pl.ds(pl.multiple_of(f * width, width), width)
            w = wdn[layer, :, :, at].reshape(hidden, width)
            p = jnp.dot(hid[...], w, preferred_element_type=jnp.float32)
            part[f] = p.astype(jnp.bfloat16).reshape(n_x, rows, width)
            send(part.at[f, eo, pl.ds(half, half)], xa.at[layer, i, 0], sends.at[4], xas.at[layer, i, 0], x(1))
            send(part.at[f, eo, pl.ds(0, half)], xa.at[layer, i, 1], sends.at[4], xas.at[layer, i, 1], x(-1))

        def merge_x(i):
            f = owner(ORDER[i])
            for side, (to, at, step) in enumerate(((ep, half, 1), (em, 0, -1))):
                await_bytes(xa.at[layer, i, side], xas.at[layer, i, side])
                old = part[f, to, at : at + half, :].astype(jnp.float32)
                new = old + xa[layer, i, side].astype(jnp.float32)
                part[f, to, at : at + half, :] = new.astype(jnp.bfloat16)
                send(part.at[f, to], xb.at[layer, i, side], sends.at[4], xbs.at[layer, i, side], x(step))

        def merge_z(i):
            delta = ORDER[i]
            f = owner(delta)
            for side in range(2):
                await_bytes(xb.at[layer, i, side], xbs.at[layer, i, side])
            total = part[f, e].astype(jnp.float32)
            for side in range(2):
                total = total + xb[layer, i, side].astype(jnp.float32)
            if delta == 0:
                for j in range(len(HUBS)):
                    await_bytes(zdest.at[layer, j], zds.at[layer, j])
                    total = total + zdest[layer, j].astype(jnp.float32)
                new = (acts[layer, m, e].astype(jnp.float32) + total).astype(jnp.bfloat16)
                out_ref[...] = new

                @pl.when(layer == 0)
                def _():
                    acts[1, m, e] = new

                return
            for s in FORWARD.get(delta, ()):
                j = LEAVES.index(delta + s)
                await_bytes(zleaf.at[layer, j], zls.at[layer, j])
                total = total + zleaf[layer, j].astype(jnp.float32)
            stage[i] = total.astype(jnp.bfloat16)
            if delta in HUBS:
                j = HUBS.index(delta)
                send(stage.at[i], zdest.at[layer, j], sends.at[5], zds.at[layer, j], z(-delta))
            else:
                j = LEAVES.index(delta)
                send(stage.at[i], zleaf.at[layer, j], sends.at[5], zls.at[layer, j], z(TO_HUB[delta]))

        last = n_mp - 1
        for t in range(n_mp + RS_LAG[1]):
            if t < n_mp:
                down(last - t)
            if 0 <= t - RS_LAG[0] < n_mp:
                merge_x(last - (t - RS_LAG[0]))
            if 0 <= t - RS_LAG[1] < n_mp:
                merge_z(last - (t - RS_LAG[1]))

        some = acts.at[layer, pl.ds(0, n_mp - 1), pl.ds(0, 1)]
        most = acts.at[layer, :, pl.ds(0, 3)]
        await_bytes(some, sends.at[0])
        await_bytes(most, sends.at[1])
        await_bytes(most, sends.at[4])
        await_bytes(some, sends.at[5])
        return carry

    lax.fori_loop(0, LAYERS, layer_step, 0)
    await_bytes(gains.at[pl.ds(0, n_mp - 1)], sends.at[2])
    await_bytes(routes.at[pl.ds(0, n_x - 1)], sends.at[3])
    for layer in range(LAYERS):
        for j in range(3):
            await_bytes(wdn.at[layer, 1], sw.at[layer, j])


def solution(mesh):
    n_mp, n_x = mesh.shape["mp"], mesh.shape["expert"]

    def body(hidden_in, norm_gain, expert_ids, gate_counts, exit_layer, w_gate, w_up, w_down):
        rows, width = hidden_in.shape
        _, _, rank, full = w_gate.shape
        tokens, bf = n_x * rows, jnp.bfloat16
        vm, dma = pltpu.VMEM, pltpu.SemaphoreType.DMA
        vmem = pl.BlockSpec(memory_space=pltpu.VMEM)
        hbm = pl.BlockSpec(memory_space=pl.ANY)
        return pl.pallas_call(
            kernel,
            out_shape=jax.ShapeDtypeStruct((rows, width), bf),
            in_specs=[vmem] * 5 + [hbm] * 3,
            out_specs=vmem,
            scratch_shapes=[
                vm((LAYERS, n_mp, n_x, rows, width), bf),
                vm((n_mp, LAYERS, width), jnp.float32),
                vm((n_x, LAYERS * n_x, 128), jnp.float32),
                vm((LAYERS, 2, 2, rank, full), bf),
                vm((LAYERS, 2, rank, full), bf),
                vm((2, tokens, 2 * rank), jnp.float32),
                vm((tokens, width), jnp.float32),
                vm((tokens, 2 * rank), bf),
                vm((n_mp, n_x, rows, width), bf),
                vm((LAYERS, n_mp, 2, rows // 2, width), bf),
                vm((LAYERS, n_mp, 2, rows, width), bf),
                vm((n_mp, rows, width), bf),
                vm((LAYERS, len(LEAVES), rows, width), bf),
                vm((LAYERS, len(HUBS), rows, width), bf),
                dma((LAYERS, n_mp)),
                dma((LAYERS, n_mp, 3)),
                dma((n_mp,)),
                dma((3,)),
                dma((LAYERS, n_mp, 2)),
                dma((LAYERS, n_mp, 2)),
                dma((LAYERS, len(LEAVES))),
                dma((LAYERS, len(HUBS))),
                dma((LAYERS, 3)),
                dma((LAYERS, 3)),
                dma((LAYERS, 3)),
                dma((6,)),
            ],
            compiler_params=pltpu.CompilerParams(
                collective_id=0, has_side_effects=True, vmem_limit_bytes=60 * 1024 * 1024
            ),
        )(
            hidden_in,
            norm_gain,
            jnp.transpose(expert_ids, (0, 2, 1)),
            jnp.transpose(gate_counts, (0, 2, 1)),
            exit_layer[None, :],
            w_gate,
            w_up,
            w_down,
        )

    in_specs = (
        P(("groups", "expert", "dp"), "mp"),
        P(None, "mp"),
        P(None, ("groups", "expert", "dp"), None),
        P(None, ("groups", "expert", "dp"), None),
        P(("groups", "expert", "dp")),
        P(None, "expert", ("mp", "dp"), None),
        P(None, "expert", ("mp", "dp"), None),
        P(None, "expert", ("mp", "dp"), None),
    )
    out_specs = P(("groups", "expert", "dp"), "mp")
    return jax.shard_map(body, mesh=mesh, in_specs=in_specs, out_specs=out_specs, check_vma=False)
```

time: 337 us -> 150 us (0.45)
  waiting for transfers between devices: 155 us -> 0 us
  Pallas kernels: 0 us -> 148 us
  blocking collectives: 106 us -> 0 us
  matrix products: 29.4 us -> 0 us
  between operations: 13.3 us -> 0.01 us
  starting transfers between devices: 12.6 us -> 0 us
  other arithmetic: 11.3 us -> 0 us
  local copies, waits for them, and re-layouts: 8.24 us -> 1.38 us
    pallas_call x0 -> x1, Pallas kernels: none -> 148 us  [body(): pl.pallas_call(kernel, out_shape=jax.ShapeDtypeStruct((rows, width), bf),...]
    reduce_scatter x2 -> x0, waiting for transfers between devices: 127 us -> none  [body(): lax.psum_scatter(partial_value.astype(jnp.bfloat16), 'mp', scatter_dimens...]
    all_gather x2 -> x0, blocking collectives: 82.5 us -> none  [rows_first(): whole, at, outs = (lax.all_gather(both, axis, axis=0, tiled=True), 0, [])]
    dot_general x8 -> x0, matrix products: 29.4 us -> none  [the longest x2 18.2 us: body(): jnp.dot(hidden, down_rows, preferred_element_type=jnp.float32)]
    all_to_all x3 -> x0, waiting for transfers between devices: 28.1 us -> none  [the longest x1 16.1 us: body(): lax.all_to_all(outgoing, 'expert', split_axis=0, concat_axis=0, tiled=True)]
    all_to_all x1 -> x0, blocking collectives: 23.9 us -> none  [body(): lax.all_to_all(outgoing, 'expert', split_axis=0, concat_axis=0, tiled=True)]
    all_to_all x3 -> x0, starting transfers between devices: 12.2 us -> none  [the longest x2 8.52 us: body(): lax.all_to_all(summed.reshape(experts, tok_rows, slice_width), 'expert',...]
    concatenate x4 -> x0, other arithmetic: 10.5 us -> none  [the longest x2 10.5 us: side_by_side(): both = jnp.concatenate(arrays, axis=along)]
  transfers between devices with their start and end apart: 7 -> 0, of which waited for: 5 -> 0; matrix products, arithmetic and copies ran while one was open for 3% -> 0% of each run, Pallas kernels for 0% -> 0%
where the time goes in v1:
time: 150 us; the launch traced here: 149 us
  Pallas kernels  148 us (99%)
    pallas_call x1, Pallas kernels, body(): pl.pallas_call(kernel, out_shape=jax.ShapeDtypeStruct((rows, width), bf),...  148 us

profile of v1, /device:TPU:40, one launch (start us, length us, event | category | flops | bytes accessed | tf_op | source)
XLA Modules:
  0.0 149.5 jit_solution(16656717913806709930)
XLA Ops:
  0.0 148.1 %shard_map.82 = bf16[64,256]{1,0:T(8,128)(2,1)} custom-call(bf16[64,256]{1,0:T(8,128)(2,1)} %cur_in.1, bf16[2,256]{1,0:T(2,128)(2,1)} %gain_in.1, s32[2,2,64]{2,1,0:T(2,128)} %bitcast.3, s32[2,2,64]{2,1,0:T(2,128)} %bitcast.4, s32[1,64]{1,0:T(1,128)} %bitcast.5, bf16[2,1,224,4096]{3,2,1,0:T(8,128)(2,1)} %wg_hbm.1, bf16[2,1,224,4096]{3,2,1,0:T(8,128)(2,1)} %wu_hbm.1, ...), custom_call_target="tpu_custom_call" | custom-call | tf_op jit(solution)/shard_map/pallas_call | solution.py:270
  148.1 1.4 copy.10

commit v2 on v1

--- a/solution.py
+++ b/solution.py
@@ -9,19 +9,41 @@
 NORM_FLOOR = 0.1
 MESH = pl.DeviceIdType.MESH
 
-ORDER = (0, 1, -1, 4, -4, 2, -2, 7, -7, 3, -3, 5, -5, 6, -6, 8)
-HUBS = (7, -7, 4, -4, 1, -1)
-FORWARD = {1: (1,), -1: (-1,), 4: (1, -1), -4: (-1, 1), 7: (1, -1), -7: (1,)}
-LEAVES = tuple(h + s for h in HUBS for s in FORWARD[h])
-TO_HUB = {h + s: -s for h in HUBS for s in FORWARD[h]}
-AG_LAG = (3, 6)
-RS_LAG = (3, 6)
+CHILDREN = {
+    0: ((4, False), (-4, False), (1, False), (-1, False)),
+    1: ((2, True),),
+    -1: ((-2, True),),
+    4: ((7, False), (5, False), (3, True)),
+    -4: ((-7, False), (-5, False), (-3, True)),
+    7: ((8, False), (6, False)),
+    -7: ((-6, False),),
+}
+PARENT = {c: p for p, cs in CHILDREN.items() for c, _ in cs}
+SINGLE = tuple(c for cs in CHILDREN.values() for c, whole in cs if not whole)
+WHOLE = tuple(c for cs in CHILDREN.values() for c, whole in cs if whole)
+ORDER = (0, *PARENT)
+STEPS = tuple(sorted({c - p for c, p in PARENT.items()} | {p - c for c, p in PARENT.items()}))
+
+
+def plan():
+    arrival = {0: 0.0, 1: 2.6, 4: 4.5, 5: 7.2, 7: 8.2, 6: 10.8, 8: 10.9}
+    arrival |= {-d: t + 0.1 for d, t in arrival.items() if d not in (0, 8)}
+    ops, start, done = [], -1.0, {}
+    for delta in sorted(arrival, key=arrival.get):
+        start = max(arrival[delta], start + 0.85)
+        done[delta] = start + 5.6
+        ops += [(arrival[delta], "z", delta), (start + 2.8, "x", delta), (done[delta], "m", delta)]
+    ops += [(done[PARENT[delta]] + 3.6, "m", delta) for delta in WHOLE]
+    return [(kind, delta) for _, kind, delta in sorted(ops)]
+
+
+PLAN = plan()
 
 
 def kernel(
     cur_in, gain_in, ids_in, counts_in, exit_in, wg_hbm, wu_hbm, wd_hbm, out_ref,
-    acts, gains, routes, wgu, wdn, acc, ssq, hid, part, xa, xb, stage, zleaf, zdest,
-    zr, xr, gr, rr, xas, xbs, zls, zds, lw, rw, sw, sends,
+    acts, gains, routes, wgu, wdn, acc, ssq, hid, part, xa, xb, stage, zin, zrow,
+    zr, xr, gr, rr, xas, xbs, zs, zrs, lw, rw, sw, sends,
 ):
     m, e, d = lax.axis_index("mp"), lax.axis_index("expert"), lax.axis_index("dp")
     n_mp, n_x = acts.shape[1], acts.shape[2]
@@ -82,48 +104,43 @@
     acts[0, m, e] = cur_in[...]
 
     barrier = pltpu.get_barrier_semaphore()
-    peers = [z(h) for h in HUBS] + [x(1), x(-1), x(2), partner]
+    peers = [z(h) for h in STEPS] + [x(1), x(-1), x(2), partner]
     for dev in peers:
         pl.semaphore_signal(barrier, inc=1, device_id=dev, device_id_type=MESH)
     pl.semaphore_wait(barrier, len(peers))
 
     def layer_step(layer, carry):
-        own = acts.at[layer, m, e]
-        for h in HUBS:
-            send(own, own, sends.at[0], zr.at[layer, ORDER.index(h)], z(h))
-
-        def spread(i):
-            block = acts.at[layer, owner(ORDER[i]), e]
+        def spread(delta):
+            i = ORDER.index(delta)
+            block = acts.at[layer, owner(delta), e]
+            for child, whole in CHILDREN.get(delta, ()):
+                if not whole:
+                    send(block, block, sends.at[0], zr.at[layer, ORDER.index(child)], z(child - delta))
             send(block, block, sends.at[1], xr.at[layer, i, 0], x(1))
             send(block, block, sends.at[1], xr.at[layer, i, 1], x(-1))
 
-        spread(0)
-
-        @pl.when(layer == 0)
-        def _():
-            for h in HUBS:
-                send(gains.at[m], gains.at[m], sends.at[2], gr.at[ORDER.index(h)], z(h))
-            for j, s in enumerate((1, -1, 2)):
-                send(routes.at[e], routes.at[e], sends.at[3], rr.at[j], x(s))
-            give_weights(0)
-
-        def take_z(i):
-            delta = ORDER[i]
-            k = owner(delta)
-            block = acts.at[layer, k, e]
-            await_bytes(block, zr.at[layer, i])
-            for s in FORWARD.get(delta, ()):
-                send(block, block, sends.at[0], zr.at[layer, ORDER.index(delta + s)], z(s))
-            spread(i)
-
             @pl.when(layer == 0)
             def _():
-                await_bytes(gains.at[k], gr.at[i])
-                for s in FORWARD.get(delta, ()):
-                    send(gains.at[k], gains.at[k], sends.at[2], gr.at[ORDER.index(delta + s)], z(s))
-
-        def take_x(i):
-            k = owner(ORDER[i])
+                gain = gains.at[owner(delta)]
+                if delta != 0:
+                    await_bytes(gain, gr.at[i])
+                for child, _ in CHILDREN.get(delta, ()):
+                    send(gain, gain, sends.at[2], gr.at[ORDER.index(child)], z(child - delta))
+
+        def take_z(delta):
+            if delta != 0:
+                await_bytes(acts.at[layer, owner(delta), e], zr.at[layer, ORDER.index(delta)])
+            spread(delta)
+            if delta == 0:
+
+                @pl.when(layer == 0)
+                def _():
+                    for j, s in enumerate((1, -1, 2)):
+                        send(routes.at[e], routes.at[e], sends.at[3], rr.at[j], x(s))
+                    give_weights(0)
+
+        def take_x(delta):
+            i, k = ORDER.index(delta), owner(delta)
             lo, hi = acts.at[layer, k, em], acts.at[layer, k, ep]
             await_bytes(lo, xr.at[layer, i, 0])
             piece = acts.at[layer, k, em, pl.ds(0, half)]
@@ -132,19 +149,31 @@
             piece = acts.at[layer, k, ep, pl.ds(half, half)]
             send(piece, piece, sends.at[1], xr.at[layer, i, 2], x(-1))
 
-        def multiply(i):
-            k = owner(ORDER[i])
-            await_bytes(acts.at[layer, k, eo], xr.at[layer, i, 2])
+        def multiply(delta, first):
+            i, k = ORDER.index(delta), owner(delta)
+            row = acts.at[layer, k]
+            if delta in WHOLE:
+                await_bytes(row, zr.at[layer, i])
+
+                @pl.when(layer == 0)
+                def _():
+                    await_bytes(gains.at[k], gr.at[i])
+
+            else:
+                await_bytes(acts.at[layer, k, eo], xr.at[layer, i, 2])
+            for child, whole in CHILDREN.get(delta, ()):
+                if whole:
+                    send(row, row, sends.at[6], zr.at[layer, ORDER.index(child)], z(child - delta))
             block = acts[layer, k].reshape(tokens, width).astype(jnp.float32)
             squares = block * block
             scaled = (block * gains[k, pl.ds(layer, 1), :]).astype(jnp.bfloat16)
             at = pl.ds(pl.multiple_of(k * width, width), width)
-            ssq[...] = squares if i == 0 else ssq[...] + squares
+            ssq[...] = squares if first else ssq[...] + squares
 
             def product(j, c):
                 w = wgu[layer, j, :, :, at].reshape(hidden, width)
                 p = lax.dot_general(scaled, w, (((1,), (1,)), ((), ())), preferred_element_type=jnp.float32)
-                acc[j] = p if i == 0 else acc[j] + p
+                acc[j] = p if first else acc[j] + p
                 return c
 
             lax.fori_loop(0, 2, product, 0)
@@ -153,16 +182,18 @@
             await_bytes(wdn.at[layer, 0], lw.at[layer, j])
             await_bytes(wdn.at[layer, 1], rw.at[layer, j])
 
-        for t in range(n_mp + AG_LAG[1]):
-            if 0 < t < n_mp:
-                take_z(t)
-            if 0 <= t - AG_LAG[0] < n_mp:
-                take_x(t - AG_LAG[0])
-            if 0 <= t - AG_LAG[1] < n_mp:
-                if t == AG_LAG[1]:
+        first = True
+        for kind, delta in PLAN:
+            if kind == "z":
+                take_z(delta)
+            elif kind == "x":
+                take_x(delta)
+            else:
+                if first:
                     weights_here(0)
                     weights_here(1)
-                multiply(t - AG_LAG[1])
+                multiply(delta, first)
+                first = False
 
         @pl.when(layer == 0)
         def _():
@@ -182,17 +213,26 @@
         hid[...] = (gate / (1.0 + jnp.exp(-gate)) * (acc[1] * inv) * weight).astype(jnp.bfloat16)
         weights_here(2)
 
-        def down(i):
-            f = owner(ORDER[i])
+        def down(delta):
+            i, f = ORDER.index(delta), owner(delta)
             at = pl.ds(pl.multiple_of(f * width, width), width)
             w = wdn[layer, :, :, at].reshape(hidden, width)
             p = jnp.dot(hid[...], w, preferred_element_type=jnp.float32)
+            for child, whole in CHILDREN.get(delta, ()):
+                if whole:
+                    j = WHOLE.index(child)
+                    await_bytes(zrow.at[layer, j], zrs.at[layer, j])
+                    p = p + zrow[layer, j].reshape(tokens, width).astype(jnp.float32)
             part[f] = p.astype(jnp.bfloat16).reshape(n_x, rows, width)
+            if delta in WHOLE:
+                j = WHOLE.index(delta)
+                send(part.at[f], zrow.at[layer, j], sends.at[7], zrs.at[layer, j], z(PARENT[delta] - delta))
+                return
             send(part.at[f, eo, pl.ds(half, half)], xa.at[layer, i, 0], sends.at[4], xas.at[layer, i, 0], x(1))
             send(part.at[f, eo, pl.ds(0, half)], xa.at[layer, i, 1], sends.at[4], xas.at[layer, i, 1], x(-1))
 
-        def merge_x(i):
-            f = owner(ORDER[i])
+        def merge_x(delta):
+            i, f = ORDER.index(delta), owner(delta)
             for side, (to, at, step) in enumerate(((ep, half, 1), (em, 0, -1))):
                 await_bytes(xa.at[layer, i, side], xas.at[layer, i, side])
                 old = part[f, to, at : at + half, :].astype(jnp.float32)
@@ -200,53 +240,43 @@
                 part[f, to, at : at + half, :] = new.astype(jnp.bfloat16)
                 send(part.at[f, to], xb.at[layer, i, side], sends.at[4], xbs.at[layer, i, side], x(step))
 
-        def merge_z(i):
-            delta = ORDER[i]
-            f = owner(delta)
+        def merge_z(delta):
+            i, f = ORDER.index(delta), owner(delta)
             for side in range(2):
                 await_bytes(xb.at[layer, i, side], xbs.at[layer, i, side])
             total = part[f, e].astype(jnp.float32)
             for side in range(2):
                 total = total + xb[layer, i, side].astype(jnp.float32)
-            if delta == 0:
-                for j in range(len(HUBS)):
-                    await_bytes(zdest.at[layer, j], zds.at[layer, j])
-                    total = total + zdest[layer, j].astype(jnp.float32)
-                new = (acts[layer, m, e].astype(jnp.float32) + total).astype(jnp.bfloat16)
-                out_ref[...] = new
-
-                @pl.when(layer == 0)
-                def _():
-                    acts[1, m, e] = new
-
+            for child, whole in CHILDREN.get(delta, ()):
+                if not whole:
+                    j = SINGLE.index(child)
+                    await_bytes(zin.at[layer, j], zs.at[layer, j])
+                    total = total + zin[layer, j].astype(jnp.float32)
+            if delta != 0:
+                j = SINGLE.index(delta)
+                stage[i] = total.astype(jnp.bfloat16)
+                send(stage.at[i], zin.at[layer, j], sends.at[5], zs.at[layer, j], z(PARENT[delta] - delta))
                 return
-            for s in FORWARD.get(delta, ()):
-                j = LEAVES.index(delta + s)
-                await_bytes(zleaf.at[layer, j], zls.at[layer, j])
-                total = total + zleaf[layer, j].astype(jnp.float32)
-            stage[i] = total.astype(jnp.bfloat16)
-            if delta in HUBS:
-                j = HUBS.index(delta)
-                send(stage.at[i], zdest.at[layer, j], sends.at[5], zds.at[layer, j], z(-delta))
+            new = (acts[layer, m, e].astype(jnp.float32) + total).astype(jnp.bfloat16)
+            out_ref[...] = new
+
+            @pl.when(layer == 0)
+            def _():
+                acts[1, m, e] = new
+
+        for kind, delta in reversed(PLAN):
+            if kind == "m":
+                down(delta)
+            elif kind == "x":
+                merge_x(delta)
             else:
-                j = LEAVES.index(delta)
-                send(stage.at[i], zleaf.at[layer, j], sends.at[5], zls.at[layer, j], z(TO_HUB[delta]))
-
-        last = n_mp - 1
-        for t in range(n_mp + RS_LAG[1]):
-            if t < n_mp:
-                down(last - t)
-            if 0 <= t - RS_LAG[0] < n_mp:
-                merge_x(last - (t - RS_LAG[0]))
-            if 0 <= t - RS_LAG[1] < n_mp:
-                merge_z(last - (t - RS_LAG[1]))
-
-        some = acts.at[layer, pl.ds(0, n_mp - 1), pl.ds(0, 1)]
-        most = acts.at[layer, :, pl.ds(0, 3)]
-        await_bytes(some, sends.at[0])
-        await_bytes(most, sends.at[1])
-        await_bytes(most, sends.at[4])
-        await_bytes(some, sends.at[5])
+                merge_z(delta)
+
+        singles = acts.at[layer, pl.ds(0, len(SINGLE)), pl.ds(0, 1)]
+        threes = acts.at[layer, pl.ds(0, len(SINGLE) + 1), pl.ds(0, 3)]
+        rows_of_four = acts.at[layer, pl.ds(0, len(WHOLE))]
+        for j, sent in ((0, singles), (1, threes), (4, threes), (5, singles), (6, rows_of_four), (7, rows_of_four)):
+            await_bytes(sent, sends.at[j])
         return carry
 
     lax.fori_loop(0, LAYERS, layer_step, 0)
@@ -285,20 +315,20 @@
                 vm((LAYERS, n_mp, 2, rows // 2, width), bf),
                 vm((LAYERS, n_mp, 2, rows, width), bf),
                 vm((n_mp, rows, width), bf),
-                vm((LAYERS, len(LEAVES), rows, width), bf),
-                vm((LAYERS, len(HUBS), rows, width), bf),
+                vm((LAYERS, len(SINGLE), rows, width), bf),
+                vm((LAYERS, len(WHOLE), n_x, rows, width), bf),
                 dma((LAYERS, n_mp)),
                 dma((LAYERS, n_mp, 3)),
                 dma((n_mp,)),
                 dma((3,)),
                 dma((LAYERS, n_mp, 2)),
                 dma((LAYERS, n_mp, 2)),
-                dma((LAYERS, len(LEAVES))),
-                dma((LAYERS, len(HUBS))),
+                dma((LAYERS, len(SINGLE))),
+                dma((LAYERS, len(WHOLE))),
                 dma((LAYERS, 3)),
                 dma((LAYERS, 3)),
                 dma((LAYERS, 3)),
-                dma((6,)),
+                dma((8,)),
             ],
             compiler_params=pltpu.CompilerParams(
                 collective_id=0, has_side_effects=True, vmem_limit_bytes=60 * 1024 * 1024

time: 150 us -> 133 us (0.89)
  Pallas kernels: 148 us -> 132 us
    pallas_call x1, Pallas kernels: 148 us -> 132 us  [body(): pl.pallas_call(kernel, out_shape=jax.ShapeDtypeStruct((rows, width), bf),...]
where the time goes in v2:
time: 133 us
  Pallas kernels  132 us (99%)
  local copies, waits for them, and re-layouts  1.38 us (1%)
    pallas_call x1, Pallas kernels, body(): pl.pallas_call(kernel, out_shape=jax.ShapeDtypeStruct((rows, width), bf),...  132 us

profile of v2, /device:TPU:40, one launch (start us, length us, event | category | flops | bytes accessed | tf_op | source)
XLA Modules:
  0.0 133.0 jit_solution(7141761627580541263)
XLA Ops:
  0.0 131.6 %shard_map.82 = bf16[64,256]{1,0:T(8,128)(2,1)} custom-call(bf16[64,256]{1,0:T(8,128)(2,1)} %cur_in.1, bf16[2,256]{1,0:T(2,128)(2,1)} %gain_in.1, s32[2,2,64]{2,1,0:T(2,128)} %bitcast.3, s32[2,2,64]{2,1,0:T(2,128)} %bitcast.4, s32[1,64]{1,0:T(1,128)} %bitcast.5, bf16[2,1,224,4096]{3,2,1,0:T(8,128)(2,1)} %wg_hbm.1, bf16[2,1,224,4096]{3,2,1,0:T(8,128)(2,1)} %wu_hbm.1, ...), custom_call_target="tpu_custom_call" | custom-call | tf_op jit(solution)/shard_map/pallas_call | solution.py:300
  131.6 1.4 %copy.10 = bf16[64,256]{1,0:T(8,128)(2,1)} copy(bf16[64,256]{1,0:T(8,128)(2,1)} %shard_map.82) | data formatting | bytes 65536

commit v3 on v2

--- a/solution.py
+++ b/solution.py
@@ -9,35 +9,43 @@
 NORM_FLOOR = 0.1
 MESH = pl.DeviceIdType.MESH
 
-CHILDREN = {
-    0: ((4, False), (-4, False), (1, False), (-1, False)),
-    1: ((2, True),),
-    -1: ((-2, True),),
-    4: ((7, False), (5, False), (3, True)),
-    -4: ((-7, False), (-5, False), (-3, True)),
-    7: ((8, False), (6, False)),
-    -7: ((-6, False),),
-}
-PARENT = {c: p for p, cs in CHILDREN.items() for c, _ in cs}
-SINGLE = tuple(c for cs in CHILDREN.values() for c, whole in cs if not whole)
-WHOLE = tuple(c for cs in CHILDREN.values() for c, whole in cs if whole)
-ORDER = (0, *PARENT)
-STEPS = tuple(sorted({c - p for c, p in PARENT.items()} | {p - c for c, p in PARENT.items()}))
-
-
-def plan():
-    arrival = {0: 0.0, 1: 2.6, 4: 4.5, 5: 7.2, 7: 8.2, 6: 10.8, 8: 10.9}
-    arrival |= {-d: t + 0.1 for d, t in arrival.items() if d not in (0, 8)}
-    ops, start, done = [], -1.0, {}
-    for delta in sorted(arrival, key=arrival.get):
-        start = max(arrival[delta], start + 0.85)
-        done[delta] = start + 5.6
-        ops += [(arrival[delta], "z", delta), (start + 2.8, "x", delta), (done[delta], "m", delta)]
-    ops += [(done[PARENT[delta]] + 3.6, "m", delta) for delta in WHOLE]
-    return [(kind, delta) for _, kind, delta in sorted(ops)]
-
-
-PLAN = plan()
+OUT = {4: (0, False), 6: (4, False), 1: (0, False), 7: (4, False), 8: (6, False), 2: (1, False), 3: (4, True), 5: (4, True)}
+BACK = {4: (0, False), 8: (4, False), 3: (0, False), 7: (4, False), 6: (4, False), 1: (0, False), 2: (1, True), 5: (4, True)}
+OUT_PLAN = (
+    ("z", 0), ("x", 0), ("z", 4), ("z", -4), ("z", 1), ("z", -1), ("x", 4), ("z", 6), ("x", -4), ("m", 0), ("x", 1), ("z", -7),
+    ("x", -1), ("z", -6), ("z", 7), ("m", 4), ("z", 2), ("m", -4), ("z", -2), ("z", 8), ("x", 6), ("x", -7), ("m", 1), ("x", 7),
+    ("x", -6), ("x", 2), ("m", -1), ("x", -2), ("m", 3), ("x", 8), ("m", 5), ("m", 6), ("m", 7), ("m", -7), ("m", 2), ("m", -6),
+    ("m", -3), ("m", -5), ("m", 8), ("m", -2),
+)
+BACK_PLAN = (
+    ("m", 8), ("m", 5), ("m", -7), ("m", 7), ("m", -5), ("m", -6), ("m", -2), ("m", 6), ("m", 2), ("x", 8), ("m", 3), ("m", -3),
+    ("m", 0), ("x", -7), ("x", 7), ("x", -6), ("x", 6), ("z", 8), ("m", 4), ("m", -4), ("x", -3), ("x", 3), ("x", 0), ("z", -7),
+    ("m", 1), ("z", 7), ("m", -1), ("z", -6), ("x", 4), ("z", 6), ("x", -4), ("x", 1), ("z", 3), ("z", -3), ("x", -1), ("z", -4),
+    ("z", 4), ("z", 1), ("z", -1), ("z", 0),
+)
+
+
+class Tree:
+    def __init__(self, half):
+        self.parent, self.whole = {}, []
+        for delta, (parent, whole) in half.items():
+            for sign in (1,) if delta == 8 else (1, -1):
+                self.parent[sign * delta] = sign * parent
+                if whole:
+                    self.whole.append(sign * delta)
+        self.single = [delta for delta in self.parent if delta not in self.whole]
+        self.order = [0, *self.parent]
+
+    def below(self, delta, whole):
+        among = self.whole if whole else self.single
+        return [c for c in among if self.parent[c] == delta]
+
+    def steps(self):
+        return {s * (c - p) for c, p in self.parent.items() for s in (1, -1)}
+
+
+OUT, BACK = Tree(OUT), Tree(BACK)
+STEPS = sorted(OUT.steps() | BACK.steps())
 
 
 def kernel(
@@ -111,11 +119,10 @@
 
     def layer_step(layer, carry):
         def spread(delta):
-            i = ORDER.index(delta)
+            i = OUT.order.index(delta)
             block = acts.at[layer, owner(delta), e]
-            for child, whole in CHILDREN.get(delta, ()):
-                if not whole:
-                    send(block, block, sends.at[0], zr.at[layer, ORDER.index(child)], z(child - delta))
+            for child in OUT.below(delta, False):
+                send(block, block, sends.at[0], zr.at[layer, OUT.order.index(child)], z(child - delta))
             send(block, block, sends.at[1], xr.at[layer, i, 0], x(1))
             send(block, block, sends.at[1], xr.at[layer, i, 1], x(-1))
 
@@ -124,12 +131,12 @@
                 gain = gains.at[owner(delta)]
                 if delta != 0:
                     await_bytes(gain, gr.at[i])
-                for child, _ in CHILDREN.get(delta, ()):
-                    send(gain, gain, sends.at[2], gr.at[ORDER.index(child)], z(child - delta))
+                for child in OUT.below(delta, False) + OUT.below(delta, True):
+                    send(gain, gain, sends.at[2], gr.at[OUT.order.index(child)], z(child - delta))
 
         def take_z(delta):
             if delta != 0:
-                await_bytes(acts.at[layer, owner(delta), e], zr.at[layer, ORDER.index(delta)])
+                await_bytes(acts.at[layer, owner(delta), e], zr.at[layer, OUT.order.index(delta)])
             spread(delta)
             if delta == 0:
 
@@ -140,7 +147,7 @@
                     give_weights(0)
 
         def take_x(delta):
-            i, k = ORDER.index(delta), owner(delta)
+            i, k = OUT.order.index(delta), owner(delta)
             lo, hi = acts.at[layer, k, em], acts.at[layer, k, ep]
             await_bytes(lo, xr.at[layer, i, 0])
             piece = acts.at[layer, k, em, pl.ds(0, half)]
@@ -150,9 +157,9 @@
             send(piece, piece, sends.at[1], xr.at[layer, i, 2], x(-1))
 
         def multiply(delta, first):
-            i, k = ORDER.index(delta), owner(delta)
+            i, k = OUT.order.index(delta), owner(delta)
             row = acts.at[layer, k]
-            if delta in WHOLE:
+            if delta in OUT.whole:
                 await_bytes(row, zr.at[layer, i])
 
                 @pl.when(layer == 0)
@@ -161,29 +168,28 @@
 
             else:
                 await_bytes(acts.at[layer, k, eo], xr.at[layer, i, 2])
-            for child, whole in CHILDREN.get(delta, ()):
-                if whole:
-                    send(row, row, sends.at[6], zr.at[layer, ORDER.index(child)], z(child - delta))
+            for child in OUT.below(delta, True):
+                send(row, row, sends.at[6], zr.at[layer, OUT.order.index(child)], z(child - delta))
             block = acts[layer, k].reshape(tokens, width).astype(jnp.float32)
             squares = block * block
             scaled = (block * gains[k, pl.ds(layer, 1), :]).astype(jnp.bfloat16)
             at = pl.ds(pl.multiple_of(k * width, width), width)
             ssq[...] = squares if first else ssq[...] + squares
 
-            def product(j, c):
+            def product(j):
                 w = wgu[layer, j, :, :, at].reshape(hidden, width)
                 p = lax.dot_general(scaled, w, (((1,), (1,)), ((), ())), preferred_element_type=jnp.float32)
                 acc[j] = p if first else acc[j] + p
-                return c
-
-            lax.fori_loop(0, 2, product, 0)
+
+            for j in range(2):
+                product(j)
 
         def weights_here(j):
             await_bytes(wdn.at[layer, 0], lw.at[layer, j])
             await_bytes(wdn.at[layer, 1], rw.at[layer, j])
 
         first = True
-        for kind, delta in PLAN:
+        for kind, delta in OUT_PLAN:
             if kind == "z":
                 take_z(delta)
             elif kind == "x":
@@ -214,25 +220,24 @@
         weights_here(2)
 
         def down(delta):
-            i, f = ORDER.index(delta), owner(delta)
+            i, f = BACK.order.index(delta), owner(delta)
             at = pl.ds(pl.multiple_of(f * width, width), width)
             w = wdn[layer, :, :, at].reshape(hidden, width)
             p = jnp.dot(hid[...], w, preferred_element_type=jnp.float32)
-            for child, whole in CHILDREN.get(delta, ()):
-                if whole:
-                    j = WHOLE.index(child)
-                    await_bytes(zrow.at[layer, j], zrs.at[layer, j])
-                    p = p + zrow[layer, j].reshape(tokens, width).astype(jnp.float32)
+            for child in BACK.below(delta, True):
+                j = BACK.whole.index(child)
+                await_bytes(zrow.at[layer, j], zrs.at[layer, j])
+                p = p + zrow[layer, j].reshape(tokens, width).astype(jnp.float32)
             part[f] = p.astype(jnp.bfloat16).reshape(n_x, rows, width)
-            if delta in WHOLE:
-                j = WHOLE.index(delta)
-                send(part.at[f], zrow.at[layer, j], sends.at[7], zrs.at[layer, j], z(PARENT[delta] - delta))
+            if delta in BACK.whole:
+                j = BACK.whole.index(delta)
+                send(part.at[f], zrow.at[layer, j], sends.at[7], zrs.at[layer, j], z(BACK.parent[delta] - delta))
                 return
             send(part.at[f, eo, pl.ds(half, half)], xa.at[layer, i, 0], sends.at[4], xas.at[layer, i, 0], x(1))
             send(part.at[f, eo, pl.ds(0, half)], xa.at[layer, i, 1], sends.at[4], xas.at[layer, i, 1], x(-1))
 
         def merge_x(delta):
-            i, f = ORDER.index(delta), owner(delta)
+            i, f = BACK.order.index(delta), owner(delta)
             for side, (to, at, step) in enumerate(((ep, half, 1), (em, 0, -1))):
                 await_bytes(xa.at[layer, i, side], xas.at[layer, i, side])
                 old = part[f, to, at : at + half, :].astype(jnp.float32)
@@ -241,21 +246,20 @@
                 send(part.at[f, to], xb.at[layer, i, side], sends.at[4], xbs.at[layer, i, side], x(step))
 
         def merge_z(delta):
-            i, f = ORDER.index(delta), owner(delta)
+            i, f = BACK.order.index(delta), owner(delta)
             for side in range(2):
                 await_bytes(xb.at[layer, i, side], xbs.at[layer, i, side])
             total = part[f, e].astype(jnp.float32)
             for side in range(2):
                 total = total + xb[layer, i, side].astype(jnp.float32)
-            for child, whole in CHILDREN.get(delta, ()):
-                if not whole:
-                    j = SINGLE.index(child)
-                    await_bytes(zin.at[layer, j], zs.at[layer, j])
-                    total = total + zin[layer, j].astype(jnp.float32)
+            for child in BACK.below(delta, False):
+                j = BACK.single.index(child)
+                await_bytes(zin.at[layer, j], zs.at[layer, j])
+                total = total + zin[layer, j].astype(jnp.float32)
             if delta != 0:
-                j = SINGLE.index(delta)
+                j = BACK.single.index(delta)
                 stage[i] = total.astype(jnp.bfloat16)
-                send(stage.at[i], zin.at[layer, j], sends.at[5], zs.at[layer, j], z(PARENT[delta] - delta))
+                send(stage.at[i], zin.at[layer, j], sends.at[5], zs.at[layer, j], z(BACK.parent[delta] - delta))
                 return
             new = (acts[layer, m, e].astype(jnp.float32) + total).astype(jnp.bfloat16)
             out_ref[...] = new
@@ -264,7 +268,7 @@
             def _():
                 acts[1, m, e] = new
 
-        for kind, delta in reversed(PLAN):
+        for kind, delta in BACK_PLAN:
             if kind == "m":
                 down(delta)
             elif kind == "x":
@@ -272,11 +276,10 @@
             else:
                 merge_z(delta)
 
-        singles = acts.at[layer, pl.ds(0, len(SINGLE)), pl.ds(0, 1)]
-        threes = acts.at[layer, pl.ds(0, len(SINGLE) + 1), pl.ds(0, 3)]
-        rows_of_four = acts.at[layer, pl.ds(0, len(WHOLE))]
-        for j, sent in ((0, singles), (1, threes), (4, threes), (5, singles), (6, rows_of_four), (7, rows_of_four)):
-            await_bytes(sent, sends.at[j])
+        for tree, at in ((OUT, (0, 1, 6)), (BACK, (5, 4, 7))):
+            await_bytes(acts.at[layer, pl.ds(0, len(tree.single)), pl.ds(0, 1)], sends.at[at[0]])
+            await_bytes(acts.at[layer, pl.ds(0, len(tree.single) + 1), pl.ds(0, 3)], sends.at[at[1]])
+            await_bytes(acts.at[layer, pl.ds(0, len(tree.whole))], sends.at[at[2]])
         return carry
 
     lax.fori_loop(0, LAYERS, layer_step, 0)
@@ -315,16 +318,16 @@
                 vm((LAYERS, n_mp, 2, rows // 2, width), bf),
                 vm((LAYERS, n_mp, 2, rows, width), bf),
                 vm((n_mp, rows, width), bf),
-                vm((LAYERS, len(SINGLE), rows, width), bf),
-                vm((LAYERS, len(WHOLE), n_x, rows, width), bf),
+                vm((LAYERS, len(BACK.single), rows, width), bf),
+                vm((LAYERS, len(BACK.whole), n_x, rows, width), bf),
                 dma((LAYERS, n_mp)),
                 dma((LAYERS, n_mp, 3)),
                 dma((n_mp,)),
                 dma((3,)),
                 dma((LAYERS, n_mp, 2)),
                 dma((LAYERS, n_mp, 2)),
-                dma((LAYERS, len(SINGLE))),
-                dma((LAYERS, len(WHOLE))),
+                dma((LAYERS, len(BACK.single))),
+                dma((LAYERS, len(BACK.whole))),
                 dma((LAYERS, 3)),
                 dma((LAYERS, 3)),
                 dma((LAYERS, 3)),

time: 133 us -> 123 us (0.925)
  Pallas kernels: 132 us -> 122 us
    pallas_call x1, Pallas kernels: 132 us -> 122 us  [body(): pl.pallas_call(kernel, out_shape=jax.ShapeDtypeStruct((rows, width), bf),...]
where the time goes in v3:
time: 123 us
  Pallas kernels  122 us (99%)
  local copies, waits for them, and re-layouts  1.38 us (1%)
    pallas_call x1, Pallas kernels, body(): pl.pallas_call(kernel, out_shape=jax.ShapeDtypeStruct((rows, width), bf),...  122 us

profile of v3, /device:TPU:40, one launch (start us, length us, event | category | flops | bytes accessed | tf_op | source)
XLA Modules:
  0.0 122.9 jit_solution(18135594850124352086)
XLA Ops:
  0.0 121.5 %shard_map.82 = bf16[64,256]{1,0:T(8,128)(2,1)} custom-call(bf16[64,256]{1,0:T(8,128)(2,1)} %cur_in.1, bf16[2,256]{1,0:T(2,128)(2,1)} %gain_in.1, s32[2,2,64]{2,1,0:T(2,128)} %bitcast.3, s32[2,2,64]{2,1,0:T(2,128)} %bitcast.4, s32[1,64]{1,0:T(1,128)} %bitcast.5, bf16[2,1,224,4096]{3,2,1,0:T(8,128)(2,1)} %wg_hbm.1, bf16[2,1,224,4096]{3,2,1,0:T(8,128)(2,1)} %wu_hbm.1, ...), custom_call_target="tpu_custom_call" | custom-call | tf_op jit(solution)/shard_map/pallas_call | solution.py:303
  121.5 1.4 %copy.10 = bf16[64,256]{1,0:T(8,128)(2,1)} copy(bf16[64,256]{1,0:T(8,128)(2,1)} %shard_map.82) | data formatting | bytes 65536

commit v4 on v3

--- a/solution.py
+++ b/solution.py
@@ -9,19 +9,19 @@
 NORM_FLOOR = 0.1
 MESH = pl.DeviceIdType.MESH
 
-OUT = {4: (0, False), 6: (4, False), 1: (0, False), 7: (4, False), 8: (6, False), 2: (1, False), 3: (4, True), 5: (4, True)}
+OUT = {4: (0, False), 6: (4, False), 2: (0, False), 8: (6, False), 1: (0, True), 3: (4, True), 5: (4, True), 7: (6, False)}
 BACK = {4: (0, False), 8: (4, False), 3: (0, False), 7: (4, False), 6: (4, False), 1: (0, False), 2: (1, True), 5: (4, True)}
+OUT_DIRECT = (4, 6, 7, 8)
+BACK_DIRECT = (1, 4, 6, 7, 8)
 OUT_PLAN = (
-    ("z", 0), ("x", 0), ("z", 4), ("z", -4), ("z", 1), ("z", -1), ("x", 4), ("z", 6), ("x", -4), ("m", 0), ("x", 1), ("z", -7),
-    ("x", -1), ("z", -6), ("z", 7), ("m", 4), ("z", 2), ("m", -4), ("z", -2), ("z", 8), ("x", 6), ("x", -7), ("m", 1), ("x", 7),
-    ("x", -6), ("x", 2), ("m", -1), ("x", -2), ("m", 3), ("x", 8), ("m", 5), ("m", 6), ("m", 7), ("m", -7), ("m", 2), ("m", -6),
-    ("m", -3), ("m", -5), ("m", 8), ("m", -2),
+    ("z", 0), ("x", 0), ("z", 4), ("z", -4), ("m", 0), ("z", 2), ("z", -2), ("z", 6), ("z", -6), ("m", 4), ("x", 2), ("x", -2),
+    ("m", -4), ("m", 1), ("m", -1), ("z", -7), ("z", 8), ("z", 7), ("m", -2), ("m", 2), ("m", -6), ("m", 3), ("m", 6), ("m", 5),
+    ("m", -7), ("m", 8), ("m", -5), ("m", -3), ("m", 7),
 )
 BACK_PLAN = (
-    ("m", 8), ("m", 5), ("m", -7), ("m", 7), ("m", -5), ("m", -6), ("m", -2), ("m", 6), ("m", 2), ("x", 8), ("m", 3), ("m", -3),
-    ("m", 0), ("x", -7), ("x", 7), ("x", -6), ("x", 6), ("z", 8), ("m", 4), ("m", -4), ("x", -3), ("x", 3), ("x", 0), ("z", -7),
-    ("m", 1), ("z", 7), ("m", -1), ("z", -6), ("x", 4), ("z", 6), ("x", -4), ("x", 1), ("z", 3), ("z", -3), ("x", -1), ("z", -4),
-    ("z", 4), ("z", 1), ("z", -1), ("z", 0),
+    ("m", 8), ("m", 5), ("m", -5), ("m", -7), ("m", 2), ("m", -3), ("m", 7), ("m", -2), ("m", 3), ("m", -6), ("m", 6), ("z", 8),
+    ("x", -3), ("m", 0), ("z", -7), ("x", 3), ("m", -4), ("z", 7), ("m", 4), ("z", -6), ("z", 6), ("m", -1), ("m", 1), ("z", -3),
+    ("z", 3), ("z", 4), ("z", -4), ("x", 0), ("z", 1), ("z", -1), ("z", 0),
 )
 
 
@@ -50,7 +50,7 @@
 
 def kernel(
     cur_in, gain_in, ids_in, counts_in, exit_in, wg_hbm, wu_hbm, wd_hbm, out_ref,
-    acts, gains, routes, wgu, wdn, acc, ssq, hid, part, xa, xb, stage, zin, zrow,
+    acts, gains, routes, wgu, wdn, acc, ssq, hid, part, xa, xb, xc, stage, zin, zrow,
     zr, xr, gr, rr, xas, xbs, zs, zrs, lw, rw, sw, sends,
 ):
     m, e, d = lax.axis_index("mp"), lax.axis_index("expert"), lax.axis_index("dp")
@@ -96,6 +96,10 @@
         for src, dst, j in weight_parts(layer):
             send(src, dst(1), sw.at[layer, j], rw.at[layer, j], partner)
 
+    barrier = pltpu.get_barrier_semaphore()
+    peers = [z(h) for h in STEPS] + [x(1), x(-1), x(2), partner]
+    for dev in peers:
+        pl.semaphore_signal(barrier, inc=1, device_id=dev, device_id_type=MESH)
     load_weights(0)
 
     lines = []
@@ -111,10 +115,6 @@
     gains[m] = gain_in[...].astype(jnp.float32)
     acts[0, m, e] = cur_in[...]
 
-    barrier = pltpu.get_barrier_semaphore()
-    peers = [z(h) for h in STEPS] + [x(1), x(-1), x(2), partner]
-    for dev in peers:
-        pl.semaphore_signal(barrier, inc=1, device_id=dev, device_id_type=MESH)
     pl.semaphore_wait(barrier, len(peers))
 
     def layer_step(layer, carry):
@@ -125,6 +125,8 @@
                 send(block, block, sends.at[0], zr.at[layer, OUT.order.index(child)], z(child - delta))
             send(block, block, sends.at[1], xr.at[layer, i, 0], x(1))
             send(block, block, sends.at[1], xr.at[layer, i, 1], x(-1))
+            if abs(delta) in OUT_DIRECT:
+                send(block, block, sends.at[1], xr.at[layer, i, 2], x(2))
 
             @pl.when(layer == 0)
             def _():
@@ -167,6 +169,9 @@
                     await_bytes(gains.at[k], gr.at[i])
 
             else:
+                if abs(delta) in OUT_DIRECT:
+                    await_bytes(acts.at[layer, k, em], xr.at[layer, i, 0])
+                    await_bytes(acts.at[layer, k, ep], xr.at[layer, i, 1])
                 await_bytes(acts.at[layer, k, eo], xr.at[layer, i, 2])
             for child in OUT.below(delta, True):
                 send(row, row, sends.at[6], zr.at[layer, OUT.order.index(child)], z(child - delta))
@@ -233,6 +238,11 @@
                 j = BACK.whole.index(delta)
                 send(part.at[f], zrow.at[layer, j], sends.at[7], zrs.at[layer, j], z(BACK.parent[delta] - delta))
                 return
+            if abs(delta) in BACK_DIRECT:
+                send(part.at[f, eo], xc.at[layer, i], sends.at[4], xas.at[layer, i, 0], x(2))
+                send(part.at[f, ep], xb.at[layer, i, 0], sends.at[4], xbs.at[layer, i, 0], x(1))
+                send(part.at[f, em], xb.at[layer, i, 1], sends.at[4], xbs.at[layer, i, 1], x(-1))
+                return
             send(part.at[f, eo, pl.ds(half, half)], xa.at[layer, i, 0], sends.at[4], xas.at[layer, i, 0], x(1))
             send(part.at[f, eo, pl.ds(0, half)], xa.at[layer, i, 1], sends.at[4], xas.at[layer, i, 1], x(-1))
 
@@ -252,6 +262,9 @@
             total = part[f, e].astype(jnp.float32)
             for side in range(2):
                 total = total + xb[layer, i, side].astype(jnp.float32)
+            if abs(delta) in BACK_DIRECT:
+                await_bytes(xc.at[layer, i], xas.at[layer, i, 0])
+                total = total + xc[layer, i].astype(jnp.float32)
             for child in BACK.below(delta, False):
                 j = BACK.single.index(child)
                 await_bytes(zin.at[layer, j], zs.at[layer, j])
@@ -317,6 +330,7 @@
                 vm((n_mp, n_x, rows, width), bf),
                 vm((LAYERS, n_mp, 2, rows // 2, width), bf),
                 vm((LAYERS, n_mp, 2, rows, width), bf),
+                vm((LAYERS, n_mp, rows, width), bf),
                 vm((n_mp, rows, width), bf),
                 vm((LAYERS, len(BACK.single), rows, width), bf),
                 vm((LAYERS, len(BACK.whole), n_x, rows, width), bf),

time: 123 us -> 117 us (0.951)
  Pallas kernels: 122 us -> 116 us
    pallas_call x1, Pallas kernels: 122 us -> 116 us  [body(): pl.pallas_call(kernel, out_shape=jax.ShapeDtypeStruct((rows, width), bf),...]
where the time goes in v4:
time: 117 us
  Pallas kernels  116 us (99%)
  local copies, waits for them, and re-layouts  1.38 us (1%)
    pallas_call x1, Pallas kernels, body(): pl.pallas_call(kernel, out_shape=jax.ShapeDtypeStruct((rows, width), bf),...  116 us

profile of v4, /device:TPU:40, one launch (start us, length us, event | category | flops | bytes accessed | tf_op | source)
XLA Modules:
  0.0 117.1 jit_solution(11886641663627363027)
XLA Ops:
  0.0 115.7 %shard_map.82 = bf16[64,256]{1,0:T(8,128)(2,1)} custom-call(bf16[64,256]{1,0:T(8,128)(2,1)} %cur_in.1, bf16[2,256]{1,0:T(2,128)(2,1)} %gain_in.1, s32[2,2,64]{2,1,0:T(2,128)} %bitcast.3, s32[2,2,64]{2,1,0:T(2,128)} %bitcast.4, s32[1,64]{1,0:T(1,128)} %bitcast.5, bf16[2,1,224,4096]{3,2,1,0:T(8,128)(2,1)} %wg_hbm.1, bf16[2,1,224,4096]{3,2,1,0:T(8,128)(2,1)} %wu_hbm.1, ...), custom_call_target="tpu_custom_call" | custom-call | tf_op jit(solution)/shard_map/pallas_call | solution.py:316
  115.7 1.4 %copy.10 = bf16[64,256]{1,0:T(8,128)(2,1)} copy(bf16[64,256]{1,0:T(8,128)(2,1)} %shard_map.82) | data formatting | bytes 65536

commit v5 on v4

--- a/solution.py
+++ b/solution.py
@@ -12,16 +12,16 @@
 OUT = {4: (0, False), 6: (4, False), 2: (0, False), 8: (6, False), 1: (0, True), 3: (4, True), 5: (4, True), 7: (6, False)}
 BACK = {4: (0, False), 8: (4, False), 3: (0, False), 7: (4, False), 6: (4, False), 1: (0, False), 2: (1, True), 5: (4, True)}
 OUT_DIRECT = (4, 6, 7, 8)
-BACK_DIRECT = (1, 4, 6, 7, 8)
+BACK_DIRECT = (1, 3, 4, 6, 7, 8)
 OUT_PLAN = (
-    ("z", 0), ("x", 0), ("z", 4), ("z", -4), ("m", 0), ("z", 2), ("z", -2), ("z", 6), ("z", -6), ("m", 4), ("x", 2), ("x", -2),
-    ("m", -4), ("m", 1), ("m", -1), ("z", -7), ("z", 8), ("z", 7), ("m", -2), ("m", 2), ("m", -6), ("m", 3), ("m", 6), ("m", 5),
+    ("z", 0), ("x", 0), ("z", 4), ("z", -4), ("z", 2), ("z", -2), ("z", 6), ("z", -6), ("m", 0), ("m", 4), ("x", 2), ("x", -2),
+    ("m", -4), ("z", -7), ("z", 8), ("z", 7), ("m", 1), ("m", -1), ("m", -2), ("m", 2), ("m", -6), ("m", 3), ("m", 6), ("m", 5),
     ("m", -7), ("m", 8), ("m", -5), ("m", -3), ("m", 7),
 )
 BACK_PLAN = (
-    ("m", 8), ("m", 5), ("m", -5), ("m", -7), ("m", 2), ("m", -3), ("m", 7), ("m", -2), ("m", 3), ("m", -6), ("m", 6), ("z", 8),
-    ("x", -3), ("m", 0), ("z", -7), ("x", 3), ("m", -4), ("z", 7), ("m", 4), ("z", -6), ("z", 6), ("m", -1), ("m", 1), ("z", -3),
-    ("z", 3), ("z", 4), ("z", -4), ("x", 0), ("z", 1), ("z", -1), ("z", 0),
+    ("m", 8), ("m", 5), ("m", -5), ("m", -7), ("m", 7), ("m", -6), ("m", 6), ("m", 2), ("m", -2), ("m", -3), ("m", 3), ("m", 0),
+    ("z", 8), ("z", -7), ("z", 7), ("m", -4), ("m", 4), ("z", -6), ("z", 6), ("x", 0), ("m", -1), ("m", 1), ("z", -3), ("z", 3),
+    ("z", -4), ("z", 4), ("z", 1), ("z", -1), ("z", 0),
 )
 
 

time: 117 us -> 117 us (level)
  no operation moved by 1% of the time
where the time goes in v5:
time: 117 us
  Pallas kernels  115 us (98%)
  local copies, waits for them, and re-layouts  1.38 us (1%)
    pallas_call x1, Pallas kernels, body(): pl.pallas_call(kernel, out_shape=jax.ShapeDtypeStruct((rows, width), bf),...  115 us

profile of v5, /device:TPU:40, one launch (start us, length us, event | category | flops | bytes accessed | tf_op | source)
XLA Modules:
  0.0 116.6 jit_solution(6633381817761929726)
XLA Ops:
  0.0 115.2 %shard_map.82 = bf16[64,256]{1,0:T(8,128)(2,1)} custom-call(bf16[64,256]{1,0:T(8,128)(2,1)} %cur_in.1, bf16[2,256]{1,0:T(2,128)(2,1)} %gain_in.1, s32[2,2,64]{2,1,0:T(2,128)} %bitcast.3, s32[2,2,64]{2,1,0:T(2,128)} %bitcast.4, s32[1,64]{1,0:T(1,128)} %bitcast.5, bf16[2,1,224,4096]{3,2,1,0:T(8,128)(2,1)} %wg_hbm.1, bf16[2,1,224,4096]{3,2,1,0:T(8,128)(2,1)} %wu_hbm.1, ...), custom_call_target="tpu_custom_call" | custom-call | tf_op jit(solution)/shard_map/pallas_call | solution.py:316
  115.2 1.4 %copy.10 = bf16[64,256]{1,0:T(8,128)(2,1)} copy(bf16[64,256]{1,0:T(8,128)(2,1)} %shard_map.82) | data formatting | bytes 65536
